TPU v7x, 32 devices: a whole 2x2x4 slice. The times are simulated.
32 devices in a mesh: expert: 4 (over x, core), shard: 8 (over z, y).
Axes of the slice: x: 2, y: 2, z: 4, core: 2. Of those that a mesh axis runs over, the one named last changes fastest.
Arguments:
- w_gate: float32 [64, 2048, 1408], P('expert', 'shard'), may hold values from -0.1875 to 0.1875
- w_up: float32 [64, 2048, 1408], P('expert', 'shard'), may hold values from -0.1875 to 0.1875
- router_weight: float32 [2048, 64], P('shard', 'expert'), may hold values from -0.125 to 0.125
- router_gain: float32 [2048], P('shard'), may hold values from 0.25 to 1.75
Outputs:
- serve_gate: bfloat16 [64, 2048, 1408], P('expert', None, 'shard')
- serve_up: bfloat16 [64, 2048, 1408], P('expert', None, 'shard')
- scale_gate: float32 [64, 1408], P('expert', 'shard')
- scale_up: float32 [64, 1408], P('expert', 'shard')
- serve_router: bfloat16 [2048, 64], replicated
All inputs are finite; a program needn't handle non-finite values. Where the computation divides by a largest or mean magnitude, that divisor is 1e-20 or more.
Results may differ from a plain program's by a relative error of at most 0.001.
Values may be sent and summed in bfloat16 or wider, within the bound.
A program may use at most 192 MiB of HBM per device.

v0:
```python
import jax
import jax.numpy as jnp
from jax import lax
from jax.sharding import PartitionSpec as P

D_MODEL = 2048


def on_device(w_gate, w_up, router_weight, router_gain):
    total_gate, total_up = lax.psum(
        (jnp.sum(jnp.abs(w_gate), axis=1), jnp.sum(jnp.abs(w_up), axis=1)), "shard"
    )
    scale_gate = total_gate / D_MODEL
    scale_up = total_up / D_MODEL
    narrow_gate, narrow_up = (
        (w_gate / jnp.expand_dims(scale_gate, 1)).astype(jnp.bfloat16),
        (w_up / jnp.expand_dims(scale_up, 1)).astype(jnp.bfloat16),
    )
    serve_gate, serve_up = (
        lax.all_to_all(narrow_gate, "shard", split_axis=2, concat_axis=1, tiled=True),
        lax.all_to_all(narrow_up, "shard", split_axis=2, concat_axis=1, tiled=True),
    )
    scale_gate = lax.dynamic_slice_in_dim(
        scale_gate, lax.axis_index("shard") * serve_gate.shape[2], serve_gate.shape[2], axis=1
    )
    scale_up = lax.dynamic_slice_in_dim(
        scale_up, lax.axis_index("shard") * serve_up.shape[2], serve_up.shape[2], axis=1
    )
    part_router = (router_weight * router_gain[:, None]).astype(jnp.bfloat16)
    row_router = lax.all_gather(part_router, "shard", axis=0, tiled=True)
    serve_router = lax.all_gather(row_router, "expert", axis=1, tiled=True)
    return (serve_gate, serve_up, scale_gate, scale_up, serve_router)


def solution(mesh):
    placed = (
        P("expert", "shard", None),
        P("expert", "shard", None),
        P("shard", "expert"),
        P("shard"),
    )
    return jax.shard_map(
        on_device,
        mesh=mesh,
        in_specs=placed,
        out_specs=(
            P("expert", None, "shard"),
            P("expert", None, "shard"),
            P("expert", "shard"),
            P("expert", "shard"),
            P(),
        ),
        check_vma=False,
    )
```

profile of v0, /device:TPU:0, one launch (start us, length us, event | category | flops | bytes accessed | tf_op | source)
XLA Modules:
  0.0 714.1 jit_solution(9484981068573006527)
XLA Ops:
  7.2 0.0 all-reduce.3.cloned.1.call-start
  7.2 16.0 %abs_reduce_fusion = (f32[16,1408]{1,0:T(8,128)}, f32[16,1408]{1,0:T(8,128)}) fusion(f32[16,256,1408]{2,1,0:T(8,128)} %param.5, f32[16,256,1408]{2,1,0:T(8,128)} %param.4), kind=kLoop, calls=%fused_computation.1 | loop fusion | flops 23023616 | bytes 46317568 | tf_op jit(solution)/shard_map/reduce_sum | solution.py:11
  23.3 0.0 all-reduce.3.cloned.1.call-update
  23.3 23.7 %copy.22 = f32[16,256,1408]{1,0,2:T(8,128)} copy(f32[16,256,1408]{2,1,0:T(8,128)} %param.5) | data formatting | bytes 46137344 | tf_op args[1]
  47.0 50.0 %all-reduce.3.cloned.1.call-done = (f32[16,1408]{1,0:T(8,128)}, f32[16,1408]{1,0:T(8,128)}) async-done(((f32[16,1408]{1,0:T(8,128)}, f32[16,1408]{1,0:T(8,128)}), (f32[16,1408]{1,0:T(8,128)}, f32[16,1408]{1,0:T(8,128)})) %all-reduce.3.cloned.1.call-update) | async-done | bytes 180240 | tf_op jit(solution)/shard_map/psum | solution.py:10
  97.0 0.9 broadcast_multiply_fusion
  97.9 0.3 copy.21
  98.1 14.2 %divide_convert_fusion = bf16[16,256,1408]{1,0,2:T(8,128)(2,1)} fusion(f32[16,256,1408]{1,0,2:T(8,128)} %copy.22, f32[16,1408]{0,1:T(8,128)S(1)} %copy.21), kind=kLoop, calls=%fused_computation | loop fusion | flops 11534336 | bytes 34693120 | tf_op jit(solution)/shard_map/convert_element_type | solution.py:17
  112.4 5.2 all-to-all-start.1
  117.6 0.0 copy-start
  117.6 23.7 %copy.18 = f32[16,256,1408]{1,0,2:T(8,128)} copy(f32[16,256,1408]{2,1,0:T(8,128)} %param.4) | data formatting | bytes 46137344 | tf_op args[0]
  141.3 0.0 copy-done
  141.3 0.3 copy.17
  141.6 0.0 copy-start.1
  141.6 0.0 copy-start.2
  141.6 14.2 %divide_convert_fusion.1 = bf16[16,256,1408]{1,0,2:T(8,128)(2,1)} fusion(f32[16,256,1408]{1,0,2:T(8,128)} %copy.18, f32[16,1408]{0,1:T(8,128)S(1)} %copy.17), kind=kLoop, calls=%fused_computation.2 | loop fusion | flops 11534336 | bytes 34693120 | tf_op jit(solution)/shard_map/convert_element_type | solution.py:16
  155.8 210.5 %all-to-all-done.1 = bf16[16,256,1408]{1,0,2:T(8,128)(2,1)} async-done(((bf16[16,256,1408]{1,0,2:T(8,128)(2,1)}), bf16[16,256,1408]{1,0,2:T(8,128)(2,1)}, u32[]{:S(2)}, u32[]{:S(2)}) %all-to-all-start.1) | async-done | bytes 11534368 | tf_op jit(solution)/shard_map/all_to_all | solution.py:21
  366.4 5.3 all-to-all-start
  371.7 0.0 copy-done.1
  371.7 0.0 copy-done.2
  371.7 269.1 %all_gather.6 = bf16[2048,16]{0,1:T(8,128)(2,1)S(1)} all-gather(bf16[256,16]{0,1:T(8,128)(2,1)S(1)} %multiply_convert_fusion), channel_id=1, replica_groups=mesh['expert'=4,'shard'=8] {'shard'}, dimensions={0}, use_global_device_ids=true | all-gather | bytes 73728 | tf_op jit(solution)/shard_map/all_gather | solution.py:30
  640.8 5.8 all_gather.7
  646.6 0.7 constant_dynamic-slice_fusion
  647.3 0.7 constant_dynamic-slice_fusion.1
  647.9 11.4 %copy.24 = bf16[16,8,256,176]{2,1,3,0:T(8,128)(2,1)} copy(bf16[16,8,256,176]{2,0,3,1:T(8,128)(2,1)} %bitcast.5) | data formatting | bytes 23068672 | tf_op jit(solution)/shard_map/all_to_all | solution.py:21
  659.3 18.0 %all_to_all.33 = bf16[16,2048,176]{1,2,0:T(8,128)(2,1)} reshape(bf16[16,8,256,176]{2,1,3,0:T(8,128)(2,1)} %copy.24) | data formatting | bytes 23068672 | tf_op jit(solution)/shard_map/all_to_all | solution.py:21
  677.3 0.0 all-to-all-done
  677.3 11.4 %copy.20 = bf16[16,8,256,176]{2,1,3,0:T(8,128)(2,1)} copy(bf16[16,8,256,176]{2,0,3,1:T(8,128)(2,1)} %bitcast.2) | data formatting | bytes 23068672 | tf_op jit(solution)/shard_map/all_to_all | solution.py:20
  688.6 18.0 %all_to_all.29 = bf16[16,2048,176]{1,2,0:T(8,128)(2,1)} reshape(bf16[16,8,256,176]{2,1,3,0:T(8,128)(2,1)} %copy.20) | data formatting | bytes 23068672 | tf_op jit(solution)/shard_map/all_to_all | solution.py:20
  706.6 0.7 copy.30
  (2 shorter events, 0.0 us)
Async XLA Ops:
  7.2 89.8 %all-reduce.3.cloned.1.call-start = ((), (), s32[]{:S(2)}) async-start(), calls=%async_computation.2 | async-start | bytes 360448 | tf_op jit(solution)/shard_map/psum | solution.py:10
  112.4 254.0 %all-to-all-start.1 = ((bf16[16,256,1408]{1,0,2:T(8,128)(2,1)}), bf16[16,256,1408]{1,0,2:T(8,128)(2,1)}, u32[]{:S(2)}, u32[]{:S(2)}) async-start(bf16[16,256,1408]{1,0,2:T(8,128)(2,1)} %divide_convert_fusion), calls=%async_computation.1 | async-start | bytes 23068672 | tf_op jit(solution)/shard_map/all_to_all | solution.py:21
  117.6 23.7 %copy-start = (f32[16,1408]{1,0:T(8,128)S(1)}, f32[16,1408]{1,0:T(8,128)}, u32[]{:S(2)}) copy-start(f32[16,1408]{1,0:T(8,128)} %get-tuple-element.5) | copy-start | bytes 270340
  141.6 230.1 %copy-start.1 = (f32[256,16]{0,1:T(8,128)S(1)}, f32[256,16]{0,1:T(8,128)}, u32[]{:S(2)}) copy-start(f32[256,16]{0,1:T(8,128)} %param.6) | copy-start | bytes 49156
  141.6 230.1 %copy-start.2 = (f32[256]{0:T(256)S(1)}, f32[256]{0:T(256)}, u32[]{:S(2)}) copy-start(f32[256]{0:T(256)} %param.7) | copy-start | bytes 3076
  366.4 310.9 %all-to-all-start = ((bf16[16,256,1408]{1,0,2:T(8,128)(2,1)}), bf16[16,256,1408]{1,0,2:T(8,128)(2,1)}, u32[]{:S(2)}, u32[]{:S(2)}) async-start(bf16[16,256,1408]{1,0,2:T(8,128)(2,1)} %divide_convert_fusion.1), calls=%async_computation | async-start | bytes 23068672 | tf_op jit(solution)/shard_map/all_to_all | solution.py:20
Sparse Core Ops, SparseCore 0:
  23.4 73.5 all-reduce.2
where the time goes:
time: 716 us; the launch traced here: 714 us
  blocking collectives  275 us (38%)
  waiting for transfers between devices  261 us (36%)
  local copies, waits for them, and re-layouts  109 us (15%)
  other arithmetic  45.4 us (6%)
  between operations  14.1 us (2%)
  starting transfers between devices  10.5 us (1%)
    all_gather x1, blocking collectives, on_device(): row_router = lax.all_gather(part_router, 'shard', axis=0, tiled=True)  269 us
    all_to_all x1, waiting for transfers between devices, on_device(): lax.all_to_all(narrow_up, 'shard', split_axis=2, concat_axis=1, tiled=True)  211 us
    psum x1, waiting for transfers between devices, on_device(): lax.psum((jnp.sum(jnp.abs(w_gate), axis=1), jnp.sum(jnp.abs(w_up), axis=1...  50 us
    unnamed x9, local copies, waits for them, and re-layouts  48.1 us
    all_to_all x2, local copies, waits for them, and re-layouts, on_device(): lax.all_to_all(narrow_gate, 'shard', split_axis=2, concat_axis=1, tiled=T...  29.3 us
    all_to_all x2, local copies, waits for them, and re-layouts, on_device(): lax.all_to_all(narrow_up, 'shard', split_axis=2, concat_axis=1, tiled=True)  29.3 us
    reduce_sum x1, other arithmetic, on_device(): jnp.sum(jnp.abs(w_up), axis=1)  16 us
  transfers between devices with their start and end apart: 3, of which 2 were waited for; matrix products, arithmetic and copies ran while one was open for 10% of the time, Pallas kernels for 0%

commit v1 on v0

v1 whole, which is shorter than its diff:
```python
import functools

import jax
import jax.numpy as jnp
from jax import lax
from jax.experimental import pallas as pl
from jax.experimental.pallas import tpu as pltpu
from jax.sharding import PartitionSpec as P

LANES = 128
SLOTS = 2


def plain(w_gate, w_up, router_weight, router_gain):
    model = w_gate.shape[1] * lax.axis_size("shard")
    total_gate, total_up = lax.psum(
        (jnp.sum(jnp.abs(w_gate), axis=1), jnp.sum(jnp.abs(w_up), axis=1)), "shard"
    )
    served = []
    scales = []
    for w, total in ((w_gate, total_gate), (w_up, total_up)):
        scale = total / model
        narrow = (w / jnp.expand_dims(scale, 1)).astype(jnp.bfloat16)
        out = lax.all_to_all(narrow, "shard", split_axis=2, concat_axis=1, tiled=True)
        served.append(out)
        scales.append(
            lax.dynamic_slice_in_dim(
                scale, lax.axis_index("shard") * out.shape[2], out.shape[2], axis=1
            )
        )
    part_router = (router_weight * router_gain[:, None]).astype(jnp.bfloat16)
    row_router = lax.all_gather(part_router, "shard", axis=0, tiled=True)
    serve_router = lax.all_gather(row_router, "expert", axis=1, tiled=True)
    return (*served, *scales, serve_router)


def kernel(
    n, groups, model,
    part_ref, router_ref, gate_ref, up_ref,
    out_gate, out_up, scale_ref, out_router,
    stage, loaded, arrived, block,
    load_sem, own_sem, sum_send, sum_recv, mean_send, mean_recv,
    col_send, col_recv, row_send, row_recv, data_send, data_recv,
):
    me = lax.axis_index("shard")
    group = lax.axis_index("expert")
    tasks, tiles, _ = part_ref.shape
    experts, rows, width = gate_ref.shape
    columns = width // n
    share = tasks // n
    heads = router_ref.shape[0]

    def to(p):
        return lax.rem(me + p, n)

    def source(p):
        return lax.rem(me + n - p, n)

    def load(w_ref, e, slot):
        return pltpu.make_async_copy(w_ref.at[e], loaded.at[slot], load_sem.at[slot])

    load(gate_ref, 0, 0).start()

    barrier = pltpu.get_barrier_semaphore()
    for p in range(1, n):
        pl.semaphore_signal(barrier, inc=1, device_id={"shard": to(p)})
    for q in range(1, groups):
        pl.semaphore_signal(
            barrier, inc=1, device_id={"expert": lax.rem(group + q, groups)}
        )
    pl.semaphore_wait(barrier, n - 1 + groups - 1)

    sums = []
    for p in range(1, n):
        copy = pltpu.make_async_remote_copy(
            src_ref=part_ref.at[pl.ds(to(p) * share, share)],
            dst_ref=arrived.at[p],
            send_sem=sum_send.at[p],
            recv_sem=sum_recv.at[p],
            device_id={"shard": to(p)},
        )
        copy.start()
        sums.append(copy)

    mine = pl.ds(pl.multiple_of(group * heads, heads), heads)
    block[mine, :] = router_ref[...]
    cols = []
    for q in range(1, groups):
        copy = pltpu.make_async_remote_copy(
            src_ref=router_ref,
            dst_ref=block.at[mine],
            send_sem=col_send.at[q],
            recv_sem=col_recv.at[q],
            device_id={"expert": lax.rem(group + q, groups)},
        )
        copy.start()
        cols.append(copy)

    total = part_ref[pl.ds(me * share, share)]
    for p in range(1, n):
        sums[p - 1].wait_recv()
        total = total + arrived[p]
    own = pl.ds(me * share, share)
    scale_ref[own] = total / model
    means = []
    for p in range(1, n):
        copy = pltpu.make_async_remote_copy(
            src_ref=scale_ref.at[own],
            dst_ref=scale_ref.at[own],
            send_sem=mean_send.at[p],
            recv_sem=mean_recv.at[p],
            device_id={"shard": to(p)},
        )
        copy.start()
        means.append(copy)
    for copy in means:
        copy.wait_recv()

    my_rows = pl.ds(pl.multiple_of(me * rows, rows), rows)

    def piece(k):
        return pl.ds(pl.multiple_of(k * columns, 16), columns)

    order = list(range(1, n))
    for w, (w_ref, out) in enumerate(((gate_ref, out_gate), (up_ref, out_up))):

        def step(e, carry, w=w, w_ref=w_ref, out=out):
            slot = lax.rem(e, SLOTS)
            task = w * experts + e

            @pl.when(e + 1 < experts)
            def _():
                load(w_ref, e + 1, lax.rem(e + 1, SLOTS)).start()

            load(w_ref, e, slot).wait()
            for t in range(tiles):
                lanes = slice(t * LANES, (t + 1) * LANES)
                inverse = 1.0 / scale_ref[task, t : t + 1, :]
                scaled = loaded[slot, :, lanes] * inverse
                stage[task, lanes, :] = scaled.T.astype(jnp.bfloat16)
            for p in order:
                pltpu.make_async_remote_copy(
                    src_ref=stage.at[task, piece(to(p))],
                    dst_ref=out.at[e, :, my_rows],
                    send_sem=data_send.at[w, p],
                    recv_sem=data_recv.at[w, p],
                    device_id={"shard": to(p)},
                ).start()
            pltpu.make_async_copy(
                stage.at[task, piece(me)], out.at[e, :, my_rows], own_sem.at[w]
            ).start()
            return carry

        lax.fori_loop(0, experts, step, 0)
        if w == 0:
            load(up_ref, 0, 0).start()
            for copy in cols:
                copy.wait_recv()
            lines = []
            for p in range(1, n):
                copy = pltpu.make_async_remote_copy(
                    src_ref=block,
                    dst_ref=out_router.at[:, my_rows],
                    send_sem=row_send.at[p],
                    recv_sem=row_recv.at[p],
                    device_id={"shard": to(p)},
                )
                copy.start()
                lines.append(copy)
            out_router[:, my_rows] = block[...]

    for copy in sums + cols + means:
        copy.wait_send()
    for copy in lines:
        copy.wait()
    for w, out in enumerate((out_gate, out_up)):
        held = pl.ds(w * experts, experts)
        pltpu.make_async_copy(
            stage.at[held, piece(me)], out.at[:, :, my_rows], own_sem.at[w]
        ).wait()
        for p in range(1, n):
            from_p = pl.ds(pl.multiple_of(source(p) * rows, rows), rows)
            both = pltpu.make_async_remote_copy(
                src_ref=stage.at[held, piece(to(p))],
                dst_ref=out.at[:, :, from_p],
                send_sem=data_send.at[w, p],
                recv_sem=data_recv.at[w, p],
                device_id={"shard": to(p)},
            )
            both.wait_send()
            both.wait_recv()


def on_device(w_gate, w_up, router_weight, router_gain):
    n, groups = lax.axis_size("shard"), lax.axis_size("expert")
    experts, rows, width = w_gate.shape
    heads = router_weight.shape[1]
    tasks, columns, model = 2 * experts, width // n, rows * n
    if rows % LANES or width % LANES or columns % 16 or tasks % n or heads % 16:
        return plain(w_gate, w_up, router_weight, router_gain)
    tiles = width // LANES
    part = jnp.concatenate(
        [jnp.sum(jnp.abs(w_gate), axis=1), jnp.sum(jnp.abs(w_up), axis=1)]
    ).reshape(tasks, tiles, LANES)
    part_router = (router_weight * router_gain[:, None]).astype(jnp.bfloat16).T
    vmem = pl.BlockSpec(memory_space=pltpu.VMEM)
    hbm = pl.BlockSpec(memory_space=pl.ANY)
    dma = pltpu.SemaphoreType.DMA
    out_gate, out_up, scale, router = pl.pallas_call(
        functools.partial(kernel, n, groups, model),
        out_shape=(
            jax.ShapeDtypeStruct((experts, columns, model), jnp.bfloat16),
            jax.ShapeDtypeStruct((experts, columns, model), jnp.bfloat16),
            jax.ShapeDtypeStruct((tasks, tiles, LANES), jnp.float32),
            jax.ShapeDtypeStruct((heads * groups, model), jnp.bfloat16),
        ),
        in_specs=[vmem, vmem, hbm, hbm],
        out_specs=(hbm, hbm, vmem, vmem),
        scratch_shapes=[
            pltpu.VMEM((tasks, width, rows), jnp.bfloat16),
            pltpu.VMEM((SLOTS, rows, width), jnp.float32),
            pltpu.VMEM((n, tasks // n, tiles, LANES), jnp.float32),
            pltpu.VMEM((heads * groups, rows), jnp.bfloat16),
            dma((SLOTS,)),
            dma((2,)),
            dma((n,)), dma((n,)),
            dma((n,)), dma((n,)),
            dma((groups,)), dma((groups,)),
            dma((n,)), dma((n,)),
            dma((2, n)), dma((2, n)),
        ],
        compiler_params=pltpu.CompilerParams(
            collective_id=0, has_side_effects=True, vmem_limit_bytes=56 * 2**20
        ),
    )(part, part_router, w_gate, w_up)
    mine = lax.dynamic_slice_in_dim(
        scale.reshape(tasks, width), lax.axis_index("shard") * columns, columns, axis=1
    )
    return (
        out_gate.swapaxes(1, 2),
        out_up.swapaxes(1, 2),
        mine[:experts],
        mine[experts:],
        router.T,
    )


def solution(mesh):
    placed = (
        P("expert", "shard", None),
        P("expert", "shard", None),
        P("shard", "expert"),
        P("shard"),
    )
    return jax.shard_map(
        on_device,
        mesh=mesh,
        in_specs=placed,
        out_specs=(
            P("expert", None, "shard"),
            P("expert", None, "shard"),
            P("expert", "shard"),
            P("expert", "shard"),
            P(),
        ),
        check_vma=False,
    )
```

time: 716 us -> 553 us (0.77)
  Pallas kernels: 0 us -> 515 us
  blocking collectives: 275 us -> 0 us
  waiting for transfers between devices: 261 us -> 0 us
  local copies, waits for them, and re-layouts: 109 us -> 19.2 us
  other arithmetic: 45.4 us -> 15.9 us
  between operations: 14.1 us -> 0.7 us
  starting transfers between devices: 10.5 us -> 0 us
    pallas_call x0 -> x1, Pallas kernels: none -> 515 us  [on_device(): pl.pallas_call(functools.partial(kernel, n, groups, model), out_shape=(ja...]
    all_gather x2 -> x0, blocking collectives: 275 us -> none  [the longest x1 269 us: on_device(): row_router = lax.all_gather(part_router, 'shard', axis=0, tiled=True)]
    all_to_all x2 -> x0, waiting for transfers between devices: 211 us -> none  [the longest x1 211 us: on_device(): lax.all_to_all(narrow_up, 'shard', split_axis=2, concat_axis=1, tiled=True)]
    all_to_all x4 -> x0, local copies, waits for them, and re-layouts: 58.6 us -> none  [the longest x2 29.3 us: on_device(): lax.all_to_all(narrow_gate, 'shard', split_axis=2, concat_axis=1, tiled=T...]
    psum x1 -> x0, waiting for transfers between devices: 50 us -> none  [on_device(): lax.psum((jnp.sum(jnp.abs(w_gate), axis=1), jnp.sum(jnp.abs(w_up), axis=1...]
    unnamed x9 -> x16, local copies, waits for them, and re-layouts: 48.1 us -> 17.7 us
    convert_element_type x3 -> x0, other arithmetic: 28.4 us -> none  [the longest x1 14.2 us: on_device(): (w_up / jnp.expand_dims(scale_up, 1)).astype(jnp.bfloat16)]
    all_to_all x2 -> x0, starting transfers between devices: 10.5 us -> none  [the longest x1 5.26 us: on_device(): lax.all_to_all(narrow_gate, 'shard', split_axis=2, concat_axis=1, tiled=T...]
  transfers between devices with their start and end apart: 3 -> 0, of which waited for: 2 -> 0; matrix products, arithmetic and copies ran while one was open for 10% -> 0% of each run, Pallas kernels for 0% -> 0%
where the time goes in v1:
time: 553 us; the launch traced here: 551 us
  Pallas kernels  515 us (93%)
  local copies, waits for them, and re-layouts  19.2 us (3%)
  other arithmetic  15.9 us (3%)
    pallas_call x1, Pallas kernels, on_device(): pl.pallas_call(functools.partial(kernel, n, groups, model), out_shape=(ja...  515 us
    unnamed x16, local copies, waits for them, and re-layouts  17.7 us
    reduce_sum x1, other arithmetic, on_device(): jnp.sum(jnp.abs(w_up), axis=1)  15.2 us

profile of v1, /device:TPU:0, one launch (start us, length us, event | category | flops | bytes accessed | tf_op | source)
XLA Modules:
  0.0 550.9 jit_solution(2449466871608512085)
XLA Ops:
  0.6 0.0 copy-start.1
  0.6 0.0 copy-start.2
  0.7 15.2 %abs_reduce_fusion = (f32[16,1408]{1,0:T(8,128)S(1)}, f32[16,1408]{1,0:T(8,128)S(1)}) fusion(f32[16,256,1408]{2,1,0:T(8,128)} %up_ref.1, f32[16,256,1408]{2,1,0:T(8,128)} %gate_ref.1), kind=kLoop, calls=%fused_computation | loop fusion | flops 23023616 | bytes 46317568 | tf_op jit(solution)/shard_map/reduce_sum | solution.py:203
  15.9 0.7 reshape.17.part_ref
  16.7 0.0 copy-done.1
  16.7 0.0 copy-done.2
  16.7 0.6 fusion.router_ref
  17.3 515.2 %shard_map.83 = (bf16[16,176,2048]{2,1,0:T(8,128)(2,1)}, bf16[16,176,2048]{2,1,0:T(8,128)(2,1)}, f32[32,11,128]{2,1,0:T(8,128)}, bf16[64,2048]{1,0:T(8,128)(2,1)}) custom-call(f32[32,11,128]{2,1,0:T(8,128)} %reshape.17.part_ref, bf16[16,256]{1,0:T(8,128)(2,1)} %fusion.router_ref, f32[16,256,1408]{2,1,0:T(8,128)} %gate_ref.1, f32[16,256,1408]{2,1,0:T(8,128)} %up_ref.1), custom_call_target="tpu_custom_call" | custom-call | tf_op jit(solution)/shard_map/pallas_call | solution.py:209
  532.5 0.0 slice-start
  532.5 1.2 copy.11
  533.7 0.7 fusion.1
  534.4 0.0 slice-start.1
  534.4 0.0 slice-start.2
  534.4 0.0 copy-start
  534.4 11.4 %copy.15 = bf16[16,2048,176]{1,2,0:T(8,128)(2,1)} copy(bf16[16,2048,176]{1,2,0:T(8,128)(2,1)} %bitcast.12) | data formatting | bytes 23068672
  545.8 0.0 slice-done
  545.8 0.0 slice-done.1
  545.8 0.0 slice-done.2
  545.8 4.4 copy.16
  550.2 0.0 copy-done
  550.2 0.7 copy.17
  (2 shorter events, 0.0 us)
Async XLA Ops:
  0.6 16.0 %copy-start.1 = (f32[256,16]{0,1:T(8,128)S(1)}, f32[256,16]{0,1:T(8,128)}, u32[]{:S(2)}) copy-start(f32[256,16]{0,1:T(8,128)} %param.6) | copy-start | bytes 49156
  0.6 16.0 %copy-start.2 = (f32[256]{0:T(256)S(1)}, f32[256]{0:T(256)}, u32[]{:S(2)}) copy-start(f32[256]{0:T(256)} %param.7) | copy-start | bytes 3076
  532.5 13.3 %slice-start = ((s8[11534336]{0:T(1024)(128)(4,1)}), s8[3145728]{0:T(1024)(128)(4,1)S(1)}, s32[]{:S(2)}) async-start(s8[11534336]{0:T(1024)(128)(4,1)} %bitcast.9), calls=%async_computation | async-start | bytes 6291456
  534.4 11.4 %slice-start.1 = ((s8[11534336]{0:T(1024)(128)(4,1)}), s8[4194304]{0:T(1024)(128)(4,1)S(1)}, s32[]{:S(2)}) async-start(s8[11534336]{0:T(1024)(128)(4,1)} %bitcast.9), calls=%async_computation.1 | async-start | bytes 8388608
  534.4 11.4 %slice-start.2 = ((s8[11534336]{0:T(1024)(128)(4,1)}), s8[4194304]{0:T(1024)(128)(4,1)S(1)}, s32[]{:S(2)}) async-start(s8[11534336]{0:T(1024)(128)(4,1)} %bitcast.9), calls=%async_computation.2 | async-start | bytes 8388608
  534.4 15.9 %copy-start = (bf16[64,2048]{1,0:T(8,128)(2,1)S(1)}, bf16[64,2048]{1,0:T(8,128)(2,1)}, u32[]{:S(2)}) copy-start(bf16[64,2048]{1,0:T(8,128)(2,1)} %get-tuple-element.12) | copy-start | bytes 786436
